TPU v7x, 32 devices: a whole 2x2x4 slice. The times are simulated.
32 devices in a mesh: seq: 8 (over z, x), mem: 4 (over y, core).
Axes of the slice: x: 2, y: 2, z: 4, core: 2. Of those that a mesh axis runs over, the one named last changes fastest.
Arguments:
- queries: bfloat16 [4096, 2048], P(('seq', 'mem')), may hold values from -6 to 6
- keys: bfloat16 [4096, 2048], P(('seq', 'mem')), may hold values from -0.52734375 to 0.52734375
- values: bfloat16 [4096, 2048], P(('seq', 'mem')), may hold values from -6 to 6
- gamma: bfloat16 [4096, 16], P(('seq', 'mem')), as said below
- rate: bfloat16 [4, 16], replicated, as said below
- route_ids: int32 [4096, 2], P(('seq', 'mem')), may hold values from 0 to 3, all different within a row; in each aligned block of 128 rows (0 to 127, 128 to 255, ...) at most 96 rows name the same one
- route_weights: float32 [4096, 2], P(('seq', 'mem')), may hold values from 0.2 to 1
- norm_gain: float32 [2048], replicated, may hold values from 0.25 to 1.75
Outputs:
- mixed_out: bfloat16 [4096, 2048], P(('seq', 'mem'))
Inputs may be any that keep to these rules, and one draw needn't show every extreme that they name: `route_ids`: each token names two different memories. The tokens of one device name one memory at most 96 times; some memory is named exactly 96 times by some device's tokens. `gamma`: Positive; from 0.5 up to 6144. `rate`: Positive; from 0.04 * 4 / 4096 up to 0.06.
All inputs are finite; a program needn't handle non-finite values.
Results may differ from a plain program's by a relative error of at most 0.0052.
Values may be sent and summed in bfloat16 or wider, within the bound.
A program may use at most 128 MiB of HBM per device.

v0:
```python
import functools

import jax
import jax.numpy as jnp
from jax import lax
from jax.experimental import pallas as pl
from jax.experimental.pallas import tpu as pltpu
from jax.sharding import PartitionSpec as P

EPSILON = 1e-06
FAR = 1e30
F32 = jnp.float32
BF16 = jnp.bfloat16


def dot(a, b, dims=((1,), (0,))):
    return lax.dot_general(a, b, (dims, ((), ())), preferred_element_type=F32)


def kernel(n, seqs, hl, mems, pair, q_ref, k_ref, v_ref, gamma_ref, rate_ref,
           ids_ref, wts_ref, gain_ref, out_ref, aux_ref,
           qbuf, kbuf, vbuf, auxb, lrm, kew, adec, atot, apart, cols, pbuf, u32, ubf, upart,
           esend, erecv, sgrp, raw, outb,
           aux_s, aux_r, tok_s, tok_r, a_s, a_r, u_s, u_r, e_s, e_r, o_s, o_r):
    me = lax.axis_index("mem")
    pos = lax.axis_index("seq")
    tok = q_ref.shape[0]
    hd = qbuf.shape[-1]
    inner = lax.rem(pos, pair)
    even = inner == 0
    mate = pos + 1 - 2 * inner
    first = pos < pair
    last = pos + pair >= seqs
    rank = lax.div(pos, pair)

    def peer(step):
        return lax.rem(me + step, n)

    def lanes(head):
        return pl.ds(pl.multiple_of(head * hd, hd), hd)

    def token_copy(t, h, dst, slot):
        src, buf = ((k_ref, kbuf), (v_ref, vbuf), (q_ref, qbuf))[t]
        return pltpu.make_async_remote_copy(
            src_ref=src.at[:, lanes(dst * hl + h)], dst_ref=buf.at[slot, h],
            send_sem=tok_s.at[t, h, dst], recv_sem=tok_r.at[t, h, slot],
            device_id={"mem": dst}, device_id_type=pl.DeviceIdType.MESH)

    def aux_copy(dst, slot):
        return pltpu.make_async_remote_copy(
            src_ref=aux_ref, dst_ref=auxb.at[slot], send_sem=aux_s.at[dst], recv_sem=aux_r.at[slot],
            device_id={"mem": dst}, device_id_type=pl.DeviceIdType.MESH)

    def a_copy():
        return pltpu.make_async_remote_copy(
            src_ref=atot, dst_ref=apart, send_sem=a_s, recv_sem=a_r,
            device_id={"seq": mate}, device_id_type=pl.DeviceIdType.MESH)

    def u_copy(h, m):
        return pltpu.make_async_remote_copy(
            src_ref=ubf.at[h, m], dst_ref=upart.at[h, m], send_sem=u_s.at[h, m], recv_sem=u_r.at[h, m],
            device_id={"seq": mate}, device_id_type=pl.DeviceIdType.MESH)

    def e_copy(h, m):
        return pltpu.make_async_remote_copy(
            src_ref=esend.at[h, m], dst_ref=erecv.at[h, m], send_sem=e_s.at[h, m], recv_sem=e_r.at[h, m],
            device_id={"seq": lax.rem(pos + pair, seqs)}, device_id_type=pl.DeviceIdType.MESH)

    def out_copy(h, dst, slot):
        return pltpu.make_async_remote_copy(
            src_ref=outb.at[h, dst], dst_ref=out_ref.at[:, lanes(slot * hl + h)],
            send_sem=o_s.at[h, dst], recv_sem=o_r.at[h, slot],
            device_id={"mem": dst}, device_id_type=pl.DeviceIdType.MESH)

    barrier = pltpu.get_barrier_semaphore()

    def greet(**where):
        pl.semaphore_signal(barrier, inc=1, device_id=where, device_id_type=pl.DeviceIdType.MESH)

    for step in range(1, n):
        greet(mem=peer(step))
    greet(seq=mate)

    @pl.when(jnp.logical_not(first))
    def _():
        greet(seq=pos - pair)

    @pl.when(jnp.logical_not(last))
    def _():
        greet(seq=pos + pair)

    row_at = lax.broadcasted_iota(jnp.int32, (tok, tok), 0)
    col_at = lax.broadcasted_iota(jnp.int32, (tok, tok), 1)
    heads = hl * n
    eye = (row_at == col_at).astype(BF16)
    aux_ref[0:heads, :] = dot(gamma_ref[...], eye, ((0,), (0,)))
    aux_ref[heads:heads + 2, :] = dot(ids_ref[...].astype(BF16), eye, ((0,), (0,)))
    aux_ref[heads + 2:heads + 4, :] = lax.dot_general(
        wts_ref[...], eye.astype(F32), (((0,), (0,)), ((), ())),
        precision=lax.Precision.HIGHEST, preferred_element_type=F32)
    aux_ref[heads + 4:, :] = jnp.zeros((aux_ref.shape[0] - heads - 4, tok), F32)

    pl.semaphore_wait(barrier, n + jnp.minimum(rank, 1) + jnp.minimum(seqs // pair - 1 - rank, 1))

    for step in range(1, n):
        aux_copy(peer(step), me).start()
    for h in range(hl):
        for t in (0, 1):
            for step in range(1, n):
                token_copy(t, h, peer(step), me).start()
    for h in range(hl):
        for step in range(1, n):
            token_copy(2, h, peer(step), me).start()

    auxb[me] = aux_ref[...]
    for h in range(hl):
        kbuf[me, h] = k_ref[:, lanes(me * hl + h)]
        vbuf[me, h] = v_ref[:, lanes(me * hl + h)]
        qbuf[me, h] = q_ref[:, lanes(me * hl + h)]

    upper = (row_at <= col_at).astype(BF16)
    for step in range(1, n):
        aux_copy(peer(step), peer(step)).wait_recv()

    table = rate_ref[...].astype(F32)
    head_at = lax.broadcasted_iota(jnp.int32, table.shape, 1)
    rates = jnp.concatenate(
        [jnp.sum(jnp.where(head_at == me * hl + h, table, 0.0), axis=1, keepdims=True) for h in range(hl)], axis=0)
    total = jnp.zeros((hl * mems, tok), F32)
    mem_at = lax.broadcasted_iota(jnp.int32, (mems, tok), 0).astype(F32)
    for j in range(n):
        ids = [auxb[j, heads + r:heads + r + 1, :] for r in (0, 1)]
        wts = [auxb[j, heads + 2 + r:heads + 3 + r, :] for r in (0, 1)]
        hit = [ids[r] == mem_at for r in (0, 1)]
        mask = jnp.logical_or(hit[0], hit[1])
        gam = [auxb[j, pl.ds(me * hl + h, 1), :] for h in range(hl)]
        picked = jnp.concatenate([jnp.where(mask, g, 0.0) for g in gam], axis=0)
        level = -rates * dot(picked.astype(BF16), upper)
        here = jnp.concatenate([jnp.where(mask, 1.0, 0.0)] * hl, axis=0) > 0.5
        end = jnp.broadcast_to(level[:, tok - 1:tok], level.shape)
        lrm[j] = jnp.where(here, level, FAR)
        kew[j] = jnp.where(here, jnp.exp(end - level), 0.0)
        adec[j] = jnp.exp(end)
        for h in range(hl):
            own = level[h * mems:(h + 1) * mems]
            ahead = own + total[h * mems:(h + 1) * mems]
            rows = [jnp.sum(jnp.where(hit[r], own, 0.0), axis=0, keepdims=True) for r in (0, 1)]
            rows += [jnp.sum(jnp.where(hit[r], ahead, 0.0), axis=0, keepdims=True) for r in (0, 1)]
            cols[j, h] = jnp.concatenate(rows + ids + wts, axis=0).T
        total = total + end
    atot[...] = jnp.exp(total)
    a_copy().start()

    def update(h):
        for j in range(n):
            @pl.when(me != j)
            def _():
                token_copy(0, h, j, j).wait_recv()
                token_copy(1, h, j, j).wait_recv()
        state = jnp.zeros((mems * hd, hd), F32)
        for j in range(n):
            turned = kbuf[j, h].astype(F32).T
            keyed = jnp.concatenate(
                [(turned * kew[j, pl.ds(h * mems + m, 1), :]).astype(BF16) for m in range(mems)], axis=0)
            fresh = dot(keyed, vbuf[j, h])
            if j > 0:
                pbuf[h, j] = state.astype(BF16)
                state = jnp.concatenate(
                    [adec[j, pl.ds(h * mems + m, 1), :] * state[m * hd:(m + 1) * hd] for m in range(mems)],
                    axis=0) + fresh
            else:
                state = fresh
        for m in range(mems):
            u32[h, m] = state[m * hd:(m + 1) * hd]
            ubf[h, m] = state[m * hd:(m + 1) * hd].astype(BF16)
            u_copy(h, m).start()

    def select(ident, parts):
        got = parts[0]
        for m in range(1, mems):
            got = jnp.where(ident == float(m), parts[m], got)
        return got

    def intra(h):
        for j in range(n):
            @pl.when(me != j)
            def _():
                token_copy(2, h, j, j).wait_recv()
        causal = row_at >= col_at
        for j in range(n):
            query, value = qbuf[j, h], vbuf[j, h]
            score = dot(query, kbuf[j, h], ((1,), (1,)))
            col = cols[j, h]
            rows = [lrm[j, pl.ds(h * mems + m, 1), :] for m in range(mems)]
            weights = []
            for r in (0, 1):
                spread = col[:, r:r + 1] - select(col[:, 4 + r:5 + r], rows)
                decay = jnp.exp(jnp.where(causal, spread, -FAR))
                weights.append((decay * score).astype(BF16))
            inside = dot(jnp.concatenate(weights, axis=0), value)
            if j > 0:
                before = [dot(query, pbuf[h, j, m * hd:(m + 1) * hd, :]) for m in range(mems)]
            for r in (0, 1):
                part = inside[r * tok:(r + 1) * tok]
                if j > 0:
                    part = part + jnp.exp(col[:, r:r + 1]) * select(col[:, 4 + r:5 + r], before)
                raw[h, j, r] = part

    def relay(h, carry):
        @pl.when(h == 0)
        def _():
            a_copy().wait_recv()

        def one(m, inside):
            mine, other = atot[pl.ds(h * mems + m, 1), :], apart[pl.ds(h * mems + m, 1), :]
            u_copy(h, m).wait_recv()

            @pl.when(first)
            def _():
                erecv[h, m] = jnp.zeros((hd, hd), BF16)

            @pl.when(jnp.logical_not(first))
            def _():
                e_copy(h, m).wait_recv()

            @pl.when(jnp.logical_not(last))
            def _():
                both = jnp.where(even, other, 1.0) * u32[h, m]
                both = both + jnp.where(even, 1.0, mine) * upart[h, m].astype(F32)
                esend[h, m] = (both + mine * other * erecv[h, m].astype(F32)).astype(BF16)
                e_copy(h, m).start()

            @pl.when(even)
            def _():
                sgrp[h, m] = erecv[h, m]

            @pl.when(jnp.logical_not(even))
            def _():
                sgrp[h, m] = (other * erecv[h, m].astype(F32) + upart[h, m].astype(F32)).astype(BF16)

            return inside

        lax.fori_loop(0, mems, one, 0)
        return carry

    def finish(h):
        gain = gain_ref[:, lanes(me * hl + h)]
        for j in range(n):
            query, col = qbuf[j, h], cols[j, h]
            before = [dot(query, sgrp[h, m]) for m in range(mems)]
            mixed = jnp.zeros((tok, hd), F32)
            for r in (0, 1):
                part = raw[h, j, r] + jnp.exp(col[:, 2 + r:3 + r]) * select(col[:, 4 + r:5 + r], before)
                scale = lax.rsqrt(jnp.mean(part * part, axis=-1, keepdims=True) + EPSILON)
                mixed = mixed + col[:, 6 + r:7 + r] * (part * scale).astype(BF16).astype(F32)
            done = (mixed * gain).astype(BF16)

            @pl.when(me == j)
            def _():
                out_ref[:, lanes(me * hl + h)] = done

            @pl.when(me != j)
            def _():
                outb[h, j] = done
                out_copy(h, j, me).start()

    def due(phase):
        return jnp.clip(jnp.maximum(phase - 1 - 2 * rank, phase - 2 * hl + 1), 0, hl)

    def phase_step(phase, carry):
        @pl.when(phase < hl)
        def _():
            update(phase)

        @pl.when(jnp.logical_and(phase >= hl, phase < 2 * hl))
        def _():
            intra(phase - hl)

        @pl.when(phase >= 2 * hl)
        def _():
            finish(phase - 2 * hl)

        lax.fori_loop(due(phase), due(phase + 1), relay, 0)
        return carry

    lax.fori_loop(0, 3 * hl, phase_step, 0)

    for step in range(1, n):
        there = peer(step)
        aux_copy(there, me).wait_send()
        for h in range(hl):
            for t in range(3):
                token_copy(t, h, there, me).wait_send()
            out_copy(h, there, me).wait_send()
            out_copy(h, there, there).wait_recv()
    a_copy().wait_send()
    for h in range(hl):
        for m in range(mems):
            u_copy(h, m).wait_send()

            @pl.when(jnp.logical_not(last))
            def _():
                e_copy(h, m).wait_send()


def body(n, seqs, queries, keys, values, gamma, rate, route_ids, route_weights, norm_gain):
    tok, feats = queries.shape
    heads = gamma.shape[1]
    mems = rate.shape[0]
    hd = feats // heads
    hl = heads // n
    pair = 2
    aux_rows = -(-(heads + 4) // 8) * 8
    vm = pltpu.VMEM
    dma = pltpu.SemaphoreType.DMA
    rows = hl * mems
    scratch = [
        vm((aux_rows, tok), F32),
        vm((n, hl, tok, hd), BF16), vm((n, hl, tok, hd), BF16), vm((n, hl, tok, hd), BF16),
        vm((n, aux_rows, tok), F32),
        vm((n, rows, tok), F32), vm((n, rows, tok), F32), vm((n, rows, tok), F32),
        vm((rows, tok), F32), vm((rows, tok), F32),
        vm((n, hl, tok, 8), F32),
        vm((hl, n, mems * hd, hd), BF16),
        vm((hl, mems, hd, hd), F32), vm((hl, mems, hd, hd), BF16), vm((hl, mems, hd, hd), BF16),
        vm((hl, mems, hd, hd), BF16), vm((hl, mems, hd, hd), BF16), vm((hl, mems, hd, hd), BF16),
        vm((hl, n, 2, tok, hd), F32),
        vm((hl, n, tok, hd), BF16),
        dma((n,)), dma((n,)), dma((3, hl, n)), dma((3, hl, n)), dma, dma,
        dma((hl, mems)), dma((hl, mems)), dma((hl, mems)), dma((hl, mems)), dma((hl, n)), dma((hl, n)),
    ]
    spec = pl.BlockSpec(memory_space=pltpu.VMEM)
    return pl.pallas_call(
        functools.partial(kernel, n, seqs, hl, mems, pair),
        out_shape=jax.ShapeDtypeStruct((tok, feats), BF16),
        in_specs=[spec] * 8,
        out_specs=spec,
        scratch_shapes=scratch,
        compiler_params=pltpu.CompilerParams(
            collective_id=0, has_side_effects=True, vmem_limit_bytes=60 * 1024 * 1024),
    )(queries, keys, values, gamma, rate, route_ids, route_weights, norm_gain.reshape(1, feats))


def solution(mesh):
    rows = P(("seq", "mem"), None)
    in_specs = (rows, rows, rows, rows, P(), rows, rows, P())
    run = functools.partial(body, mesh.shape["mem"], mesh.shape["seq"])
    return jax.shard_map(run, mesh=mesh, in_specs=in_specs, out_specs=rows, check_vma=False)
```

profile of v0, /device:TPU:29, one launch (start us, length us, event | category | flops | bytes accessed | tf_op | source)
XLA Modules:
  0.0 45.6 jit_solution(14041012522894758250)
XLA Ops:
  0.0 0.0 copy-start
  0.0 1.4 %copy.9.gamma_ref = bf16[128,16]{1,0:T(8,128)(2,1)} copy(bf16[128,16]{0,1:T(8,128)(2,1)} %param.11) | data formatting | bytes 8192 | tf_op args[3]
  1.4 0.0 copy-done
  1.4 0.0 copy-start.1
  1.4 0.7 %copy.10.ids_ref = s32[128,2]{1,0:T(8,128)} copy(s32[128,2]{0,1:T(2,128)S(1)} %copy-done) | data formatting | bytes 2048 | tf_op args[5]
  2.2 0.0 copy-done.1
  2.2 0.7 %copy.11.wts_ref = f32[128,2]{1,0:T(8,128)} copy(f32[128,2]{0,1:T(2,128)S(1)} %copy-done.1) | data formatting | bytes 2048 | tf_op args[6]
  2.9 40.9 %shard_map.82 = bf16[128,2048]{1,0:T(8,128)(2,1)} custom-call(bf16[128,2048]{1,0:T(8,128)(2,1)} %q_ref.1, bf16[128,2048]{1,0:T(8,128)(2,1)} %k_ref.1, bf16[128,2048]{1,0:T(8,128)(2,1)} %v_ref.1, bf16[128,16]{1,0:T(8,128)(2,1)} %copy.9.gamma_ref, bf16[4,16]{1,0:T(4,128)(2,1)} %rate_ref.1, s32[128,2]{1,0:T(8,128)} %copy.10.ids_ref, f32[128,2]{1,0:T(8,128)} %copy.11.wts_ref, ...), custom_call_target="tpu_custom_call" | custom-call | tf_op jit(solution)/shard_map/pallas_call | solution.py:333
  43.8 1.9 %copy.13 = bf16[128,2048]{1,0:T(8,128)(2,1)} copy(bf16[128,2048]{1,0:T(8,128)(2,1)} %shard_map.82) | data formatting | bytes 1048576
Async XLA Ops:
  0.0 1.4 %copy-start = (s32[128,2]{0,1:T(2,128)S(1)}, s32[128,2]{0,1:T(2,128)}, u32[]{:S(2)}) copy-start(s32[128,2]{0,1:T(2,128)} %param.13) | copy-start | bytes 3076
  1.4 0.7 %copy-start.1 = (f32[128,2]{0,1:T(2,128)S(1)}, f32[128,2]{0,1:T(2,128)}, u32[]{:S(2)}) copy-start(f32[128,2]{0,1:T(2,128)} %param.14) | copy-start | bytes 3076
where the time goes:
time: 46.1 us; the launch traced here: 45.6 us
  Pallas kernels  40.9 us (89%)
  local copies, waits for them, and re-layouts  4.77 us (10%)
    pallas_call x1, Pallas kernels, body(): pl.pallas_call(functools.partial(kernel, n, seqs, hl, mems, pair), out_sh...  40.9 us
    unnamed x8, local copies, waits for them, and re-layouts  4.77 us

commit v1 on v0

v1 whole, which is shorter than its diff:
```python
import functools

import jax
import jax.numpy as jnp
from jax import lax
from jax.experimental import pallas as pl
from jax.experimental.pallas import tpu as pltpu
from jax.sharding import PartitionSpec as P

EPSILON = 1e-06
FAR = 1e30
F32 = jnp.float32
BF16 = jnp.bfloat16
MESH = pl.DeviceIdType.MESH

KEYS_AT = 6400
HEAD_STEP = 2860
QUERY_STEP = 1430
RELAY_AT = 9200
RELAY_STEP = 700
HOP = 2350
UPDATE_NS = 450
INTRA_NS = 250
FINISH_NS = 600


def dot(a, b, dims=((1,), (0,))):
    return lax.dot_general(a, b, (dims, ((), ())), preferred_element_type=F32)


def kernel(n, seqs, hl, mems, pair, q_ref, k_ref, v_ref, gamma_ref, rate_ref,
           ids_ref, wts_ref, gain_ref, out_ref,
           qbuf, kbuf, vbuf, gbuf, ibuf, wbuf, ratev, gainv, lrm, kew, adec, atot, apart, cols, wide, maskb,
           pbuf, xbuf, u32, ubf, upart, esend, erecv, sgrp, raw, outb,
           aux_s, aux_r, tok_s, tok_r, loc_s, a_s, a_r, u_s, u_r, e_s, e_r, o_s, o_r, own_s):
    me = lax.axis_index("mem")
    pos = lax.axis_index("seq")
    tok = qbuf.shape[2]
    hd = qbuf.shape[3]
    heads = gbuf.shape[1]
    inner = lax.rem(pos, pair)
    even = inner == 0
    mate = pos + 1 - 2 * inner
    first = pos < pair
    last = pos + pair >= seqs
    rank = lax.div(pos, pair)

    def twin(device):
        return device + 1 - 2 * lax.rem(device, 2)

    near = [twin(me)]
    away = []
    for step in range(1, n // 2):
        there = lax.rem(me + 2 * step, n)
        away += [there, twin(there)]
    peers = away + near

    def lanes(head):
        return pl.ds(pl.multiple_of(head * hd, hd), hd)

    def token_copy(t, h, dst, slot):
        src, buf = ((k_ref, kbuf), (v_ref, vbuf), (q_ref, qbuf))[t]
        return pltpu.make_async_remote_copy(
            src_ref=src.at[:, lanes(dst * hl + h)], dst_ref=buf.at[slot, h],
            send_sem=tok_s.at[t, h, dst], recv_sem=tok_r.at[t, h, slot],
            device_id={"mem": dst}, device_id_type=MESH)

    def own_token(t, h):
        src, buf = ((k_ref, kbuf), (v_ref, vbuf), (q_ref, qbuf))[t]
        return pltpu.make_async_copy(src.at[:, lanes(me * hl + h)], buf.at[me, h], tok_s.at[t, h, me])

    def aux_copy(t, dst, slot):
        src, buf = ((gamma_ref, gbuf), (ids_ref, ibuf), (wts_ref, wbuf))[t]
        return pltpu.make_async_remote_copy(
            src_ref=src, dst_ref=buf.at[slot], send_sem=aux_s.at[t, dst], recv_sem=aux_r.at[t, slot],
            device_id={"mem": dst}, device_id_type=MESH)

    def own_aux(t):
        src, buf = ((gamma_ref, gbuf), (ids_ref, ibuf), (wts_ref, wbuf))[t]
        return pltpu.make_async_copy(src, buf.at[me], aux_s.at[t, me])

    def local_copy(t):
        src, buf = ((rate_ref, ratev), (gain_ref, gainv))[t]
        return pltpu.make_async_copy(src, buf, loc_s.at[t])

    def a_copy():
        return pltpu.make_async_remote_copy(
            src_ref=atot, dst_ref=apart, send_sem=a_s, recv_sem=a_r,
            device_id={"seq": mate}, device_id_type=MESH)

    def u_copy(h, m):
        return pltpu.make_async_remote_copy(
            src_ref=ubf.at[h, m], dst_ref=upart.at[h, m], send_sem=u_s.at[h, m], recv_sem=u_r.at[h, m],
            device_id={"seq": mate}, device_id_type=MESH)

    def e_copy(h, m):
        return pltpu.make_async_remote_copy(
            src_ref=esend.at[h, m], dst_ref=erecv.at[h, m], send_sem=e_s.at[h, m], recv_sem=e_r.at[h, m],
            device_id={"seq": lax.rem(pos + pair, seqs)}, device_id_type=MESH)

    def out_copy(h, dst, slot):
        return pltpu.make_async_remote_copy(
            src_ref=outb.at[h, dst], dst_ref=out_ref.at[:, lanes(slot * hl + h)],
            send_sem=o_s.at[h, dst], recv_sem=o_r.at[h, slot],
            device_id={"mem": dst}, device_id_type=MESH)

    def own_out(h):
        return pltpu.make_async_copy(outb.at[h, me], out_ref.at[:, lanes(me * hl + h)], own_s.at[h])

    barrier = pltpu.get_barrier_semaphore()

    def greet(**where):
        pl.semaphore_signal(barrier, inc=1, device_id=where, device_id_type=MESH)

    for there in peers:
        greet(mem=there)
    greet(seq=mate)

    @pl.when(jnp.logical_not(first))
    def _():
        greet(seq=pos - pair)

    @pl.when(jnp.logical_not(last))
    def _():
        greet(seq=pos + pair)

    for t in range(3):
        own_aux(t).start()
    for t in range(2):
        local_copy(t).start()
    for h in range(hl):
        for t in range(3):
            own_token(t, h).start()

    pl.semaphore_wait(barrier, n + jnp.minimum(rank, 1) + jnp.minimum(seqs // pair - 1 - rank, 1))

    for there in peers:
        for t in range(3):
            aux_copy(t, there, me).start()
    for h in range(hl):
        for t in (0, 1):
            for there in peers:
                token_copy(t, h, there, me).start()
    for h in range(hl):
        for there in peers:
            token_copy(2, h, there, me).start()

    row_at = lax.broadcasted_iota(jnp.int32, (tok, tok), 0)
    col_at = lax.broadcasted_iota(jnp.int32, (tok, tok), 1)
    rows = hl * mems

    local_copy(0).wait()
    table = ratev[...].astype(F32)
    head_at = lax.broadcasted_iota(jnp.int32, table.shape, 1)
    rates = jnp.concatenate(
        [jnp.sum(jnp.where(head_at == me * hl + h, table, 0.0), axis=1, keepdims=True) for h in range(hl)], axis=0)
    upper = (row_at <= col_at).astype(BF16)
    chosen = me * hl + lax.div(lax.broadcasted_iota(jnp.int32, (rows, heads), 0), mems)
    pick = (lax.broadcasted_iota(jnp.int32, (rows, heads), 1) == chosen).astype(BF16)
    for t in range(3):
        own_aux(t).wait()
        for there in peers:
            aux_copy(t, there, there).wait_recv()

    total = jnp.zeros((rows, tok), F32)
    mem_at = lax.rem(lax.broadcasted_iota(jnp.int32, (rows, tok), 0), mems)
    for j in range(n):
        ids = ibuf[j]
        hit = [ids[r:r + 1, :] == mem_at for r in (0, 1)]
        here = jnp.logical_or(hit[0], hit[1])
        picked = jnp.where(here, dot(pick, gbuf[j]), 0.0)
        level = -rates * dot(picked.astype(BF16), upper)
        end = jnp.broadcast_to(level[:, tok - 1:tok], level.shape)
        lrm[j] = jnp.where(here, level, FAR)
        kew[j] = jnp.where(here, jnp.exp(end - level), 0.0)
        adec[j] = jnp.exp(end)
        for h in range(hl):
            part = slice(h * mems, (h + 1) * mems)
            own = level[part]
            ahead = own + total[part]
            levels = [jnp.sum(jnp.where(hit[r][part], own, 0.0), axis=0, keepdims=True) for r in (0, 1)]
            aheads = [jnp.sum(jnp.where(hit[r][part], ahead, 0.0), axis=0, keepdims=True) for r in (0, 1)]
            stack = levels + [jnp.exp(x) for x in levels] + [jnp.exp(x) for x in aheads]
            cols[j, h] = jnp.concatenate(stack + [jnp.zeros((2, tok), F32)], axis=0).T
        total = total + end
        side = jnp.concatenate([ids.astype(F32), wbuf[j], jnp.zeros((4, tok), F32)], axis=0).T
        for c in range(4):
            wide[j, c] = jnp.broadcast_to(side[:, c:c + 1], (tok, hd))
        for r in (0, 1):
            for m in range(mems):
                maskb[j, r, m] = (side[:, r:r + 1] == float(m)).astype(F32).astype(BF16) * jnp.ones((tok, hd), BF16)
    atot[...] = jnp.exp(total)
    a_copy().start()
    for h in range(hl):
        pbuf[h, 0] = jnp.zeros((mems * hd, hd), BF16)

    def update(h):
        for t in (0, 1):
            own_token(t, h).wait()
            for there in peers:
                token_copy(t, h, there, there).wait_recv()
        state = jnp.zeros((mems * hd, hd), F32)
        for j in range(n):
            turned = kbuf[j, h].astype(F32).T
            keyed = jnp.concatenate(
                [(turned * kew[j, pl.ds(h * mems + m, 1), :]).astype(BF16) for m in range(mems)], axis=0)
            fresh = dot(keyed, vbuf[j, h])
            if j > 0:
                pbuf[h, j] = state.astype(BF16)
                state = jnp.concatenate(
                    [adec[j, pl.ds(h * mems + m, 1), :] * state[m * hd:(m + 1) * hd] for m in range(mems)],
                    axis=0) + fresh
            else:
                state = fresh
        for m in range(mems):
            u32[h, m] = state[m * hd:(m + 1) * hd]
            ubf[h, m] = state[m * hd:(m + 1) * hd].astype(BF16)
            u_copy(h, m).start()

    causal = row_at >= col_at

    def intra(h, j):
        query, value = qbuf[j, h], vbuf[j, h]
        score = dot(query, kbuf[j, h], ((1,), (1,)))
        query32 = query.astype(F32)
        col = cols[j, h]
        levels = [lrm[j, pl.ds(h * mems + m, 1), :] for m in range(mems)]
        left = []
        for r in (0, 1):
            ident = wide[j, r]
            level = levels[0]
            for m in range(1, mems):
                level = jnp.where(ident == float(m), levels[m], level)
            decay = jnp.exp(jnp.where(causal, col[:, r:r + 1] - level, -FAR))
            near_query = (query32 * col[:, 2 + r:3 + r]).astype(BF16)
            far_query = (query32 * col[:, 4 + r:5 + r]).astype(BF16)
            left.append(jnp.concatenate(
                [(decay * score).astype(BF16)] + [near_query * maskb[j, r, m] for m in range(mems)], axis=1))
            for m in range(mems):
                xbuf[h, j, r * tok:(r + 1) * tok, m * hd:(m + 1) * hd] = far_query * maskb[j, r, m]
        raw[h, j] = dot(jnp.concatenate(left, axis=0), jnp.concatenate([value, pbuf[h, j]], axis=0))

    def relay(unit, carry):
        h = lax.div(unit, mems)
        m = lax.rem(unit, mems)

        @pl.when(unit == 0)
        def _():
            a_copy().wait_recv()

        mine, other = atot[pl.ds(unit, 1), :], apart[pl.ds(unit, 1), :]
        u_copy(h, m).wait_recv()

        @pl.when(first)
        def _():
            erecv[h, m] = jnp.zeros((hd, hd), BF16)

        @pl.when(jnp.logical_not(first))
        def _():
            e_copy(h, m).wait_recv()

        @pl.when(jnp.logical_not(last))
        def _():
            both = jnp.where(even, other, 1.0) * u32[h, m]
            both = both + jnp.where(even, 1.0, mine) * upart[h, m].astype(F32)
            esend[h, m] = (both + mine * other * erecv[h, m].astype(F32)).astype(BF16)
            e_copy(h, m).start()

        @pl.when(even)
        def _():
            sgrp[h, m] = erecv[h, m]

        @pl.when(jnp.logical_not(even))
        def _():
            sgrp[h, m] = (other * erecv[h, m].astype(F32) + upart[h, m].astype(F32)).astype(BF16)

        return carry

    def finish(h, j):
        gain = gainv[:, lanes(me * hl + h)]
        state = jnp.concatenate([sgrp[h, m] for m in range(mems)], axis=0)
        whole = raw[h, j] + dot(xbuf[h, j], state)
        mixed = jnp.zeros((tok, hd), F32)
        for r in (0, 1):
            part = whole[r * tok:(r + 1) * tok]
            scale = lax.rsqrt(jnp.mean(part * part, axis=-1, keepdims=True) + EPSILON)
            mixed = mixed + wide[j, 2 + r] * (part * scale).astype(BF16).astype(F32)
        outb[h, j] = (mixed * gain).astype(BF16)

    done = [0]

    def catch_up(now, low, high):
        upto = jnp.clip(lax.div(now - RELAY_AT - rank * HOP + 100 * RELAY_STEP, RELAY_STEP) - 99,
                        low * mems, high * mems)
        lax.fori_loop(done[0], upto, relay, 0)
        done[0] = upto

    for h in range(hl):
        update(h)
        now = KEYS_AT + h * HEAD_STEP + UPDATE_NS
        catch_up(now, 0, h)
        own_token(2, h).wait()
        token_copy(2, h, near[0], near[0]).wait_recv()
        for j in [me] + near:
            intra(h, j)
            now += INTRA_NS
            catch_up(now, 0, h + 1)
        if h + 1 < hl:
            catch_up(KEYS_AT + (h + 1) * HEAD_STEP, 0, h + 1)

    def finish_all(h):
        for there in peers:
            finish(h, there)
            out_copy(h, there, me).start()
        finish(h, me)
        own_out(h).start()

    local_copy(1).wait()
    queries_at = KEYS_AT + (hl - 1) * HEAD_STEP + QUERY_STEP
    for h in range(hl):
        catch_up(queries_at + h * QUERY_STEP, max(h - 1, 0), hl)
        for i, there in enumerate(away):
            token_copy(2, h, there, there).wait_recv()
            intra(h, there)
            catch_up(queries_at + h * QUERY_STEP + (i + 1) * INTRA_NS, max(h - 1, 0), hl)
        if h == 1:
            catch_up(queries_at + h * QUERY_STEP + 2 * INTRA_NS, 1, hl)
            finish_all(0)
    for h in range(1 if hl > 1 else 0, hl):
        catch_up(queries_at + hl * QUERY_STEP + h * FINISH_NS, h + 1, hl)
        finish_all(h)

    for h in range(hl):
        own_out(h).wait()
    for there in peers:
        for t in range(3):
            aux_copy(t, there, me).wait_send()
        for h in range(hl):
            for t in range(3):
                token_copy(t, h, there, me).wait_send()
            out_copy(h, there, me).wait_send()
            out_copy(h, there, there).wait_recv()
    a_copy().wait_send()
    for h in range(hl):
        for m in range(mems):
            u_copy(h, m).wait_send()

            @pl.when(jnp.logical_not(last))
            def _():
                e_copy(h, m).wait_send()


def body(n, seqs, queries, keys, values, gamma, rate, route_ids, route_weights, norm_gain):
    tok, feats = queries.shape
    heads = gamma.shape[1]
    mems = rate.shape[0]
    hd = feats // heads
    hl = heads // n
    pair = 2
    vm = pltpu.VMEM
    dma = pltpu.SemaphoreType.DMA
    rows = hl * mems
    scratch = [
        vm((n, hl, tok, hd), BF16), vm((n, hl, tok, hd), BF16), vm((n, hl, tok, hd), BF16),
        vm((n, heads, tok), BF16), vm((n, 2, tok), jnp.int32), vm((n, 2, tok), F32),
        vm(rate.shape, BF16), vm((1, feats), F32),
        vm((n, rows, tok), F32), vm((n, rows, tok), F32), vm((n, rows, tok), F32),
        vm((rows, tok), F32), vm((rows, tok), F32),
        vm((n, hl, tok, 8), F32), vm((n, 4, tok, hd), F32), vm((n, 2, mems, tok, hd), BF16),
        vm((hl, n, mems * hd, hd), BF16), vm((hl, n, 2 * tok, mems * hd), BF16),
        vm((hl, mems, hd, hd), F32), vm((hl, mems, hd, hd), BF16), vm((hl, mems, hd, hd), BF16),
        vm((hl, mems, hd, hd), BF16), vm((hl, mems, hd, hd), BF16), vm((hl, mems, hd, hd), BF16),
        vm((hl, n, 2 * tok, hd), F32),
        vm((hl, n, tok, hd), BF16),
        dma((3, n)), dma((3, n)), dma((3, hl, n)), dma((3, hl, n)), dma((2,)), dma, dma,
        dma((hl, mems)), dma((hl, mems)), dma((hl, mems)), dma((hl, mems)), dma((hl, n)), dma((hl, n)), dma((hl,)),
    ]
    spec = pl.BlockSpec(memory_space=pl.ANY)
    return pl.pallas_call(
        functools.partial(kernel, n, seqs, hl, mems, pair),
        out_shape=jax.ShapeDtypeStruct((tok, feats), BF16),
        in_specs=[spec] * 8,
        out_specs=spec,
        scratch_shapes=scratch,
        compiler_params=pltpu.CompilerParams(
            collective_id=0, has_side_effects=True, vmem_limit_bytes=60 * 1024 * 1024),
    )(queries, keys, values, gamma.T, rate, route_ids.T, route_weights.T, norm_gain.reshape(1, feats))


def solution(mesh):
    rows = P(("seq", "mem"), None)
    in_specs = (rows, rows, rows, rows, P(), rows, rows, P())
    run = functools.partial(body, mesh.shape["mem"], mesh.shape["seq"])
    return jax.shard_map(run, mesh=mesh, in_specs=in_specs, out_specs=rows, check_vma=False)
```

time: 46.1 us -> 39.6 us (0.86)
  Pallas kernels: 40.9 us -> 37.5 us
  local copies, waits for them, and re-layouts: 4.77 us -> 1.88 us
    pallas_call x1, Pallas kernels: 40.9 us -> 37.5 us  [body(): pl.pallas_call(functools.partial(kernel, n, seqs, hl, mems, pair), out_sh...]
    unnamed x8 -> x1, local copies, waits for them, and re-layouts: 4.77 us -> 1.88 us
where the time goes in v1:
time: 39.6 us; the launch traced here: 39.4 us
  Pallas kernels  37.5 us (95%)
  local copies, waits for them, and re-layouts  1.88 us (5%)
    pallas_call x1, Pallas kernels, body(): pl.pallas_call(functools.partial(kernel, n, seqs, hl, mems, pair), out_sh...  37.5 us
    unnamed x1, local copies, waits for them, and re-layouts  1.88 us

profile of v1, /device:TPU:29, one launch (start us, length us, event | category | flops | bytes accessed | tf_op | source)
XLA Modules:
  0.0 39.4 jit_solution(1534881942922575934)
XLA Ops:
  0.0 37.5 %shard_map.82 = bf16[128,2048]{1,0:T(8,128)(2,1)} custom-call(bf16[128,2048]{1,0:T(8,128)(2,1)} %q_ref.1, bf16[128,2048]{1,0:T(8,128)(2,1)} %k_ref.1, bf16[128,2048]{1,0:T(8,128)(2,1)} %v_ref.1, bf16[16,128]{1,0:T(8,128)(2,1)} %bitcast.5, bf16[4,16]{1,0:T(4,128)(2,1)} %rate_ref.1, s32[2,128]{1,0:T(2,128)} %bitcast.6, f32[2,128]{1,0:T(2,128)} %bitcast.7, ...), custom_call_target="tpu_custom_call" | custom-call | tf_op jit(solution)/shard_map/pallas_call | solution.py:379
  37.5 1.9 %copy.10 = bf16[128,2048]{1,0:T(8,128)(2,1)} copy(bf16[128,2048]{1,0:T(8,128)(2,1)} %shard_map.82) | data formatting | bytes 1048576

commit v2 on v1

--- a/solution.py
+++ b/solution.py
@@ -1,4 +1,5 @@
 import functools
+import math
 
 import jax
 import jax.numpy as jnp
@@ -13,14 +14,15 @@
 BF16 = jnp.bfloat16
 MESH = pl.DeviceIdType.MESH
 
-KEYS_AT = 6400
+KEYS_AT = 8400
 HEAD_STEP = 2860
 QUERY_STEP = 1430
-RELAY_AT = 9200
-RELAY_STEP = 700
-HOP = 2350
+EARLY_AT = 8850
+LATE_AT = 12000
+PIECE_STEP = 700
+HOP = 1900
 UPDATE_NS = 450
-INTRA_NS = 250
+INTRA_NS = 360
 FINISH_NS = 600
 
 
@@ -54,6 +56,8 @@
         there = lax.rem(me + 2 * step, n)
         away += [there, twin(there)]
     peers = away + near
+    turned_later = mems // 2
+    direct = mems - turned_later
 
     def lanes(head):
         return pl.ds(pl.multiple_of(head * hd, hd), hd)
@@ -214,8 +218,9 @@
                 state = fresh
         for m in range(mems):
             u32[h, m] = state[m * hd:(m + 1) * hd]
-            ubf[h, m] = state[m * hd:(m + 1) * hd].astype(BF16)
-            u_copy(h, m).start()
+            if m < direct:
+                ubf[h, m] = state[m * hd:(m + 1) * hd].astype(BF16)
+                u_copy(h, m).start()
 
     causal = row_at >= col_at
 
@@ -240,17 +245,7 @@
                 xbuf[h, j, r * tok:(r + 1) * tok, m * hd:(m + 1) * hd] = far_query * maskb[j, r, m]
         raw[h, j] = dot(jnp.concatenate(left, axis=0), jnp.concatenate([value, pbuf[h, j]], axis=0))
 
-    def relay(unit, carry):
-        h = lax.div(unit, mems)
-        m = lax.rem(unit, mems)
-
-        @pl.when(unit == 0)
-        def _():
-            a_copy().wait_recv()
-
-        mine, other = atot[pl.ds(unit, 1), :], apart[pl.ds(unit, 1), :]
-        u_copy(h, m).wait_recv()
-
+    def receive(h, m):
         @pl.when(first)
         def _():
             erecv[h, m] = jnp.zeros((hd, hd), BF16)
@@ -259,20 +254,52 @@
         def _():
             e_copy(h, m).wait_recv()
 
+    def relay_early(unit, carry):
+        h = lax.div(unit, turned_later)
+        m = direct + lax.rem(unit, turned_later)
+        mine, other = atot[pl.ds(h * mems + m, 1), :], apart[pl.ds(h * mems + m, 1), :]
+        receive(h, m)
+        before = erecv[h, m].astype(F32)
+        fresh = u32[h, m]
+
         @pl.when(jnp.logical_not(last))
         def _():
-            both = jnp.where(even, other, 1.0) * u32[h, m]
-            both = both + jnp.where(even, 1.0, mine) * upart[h, m].astype(F32)
-            esend[h, m] = (both + mine * other * erecv[h, m].astype(F32)).astype(BF16)
+            esend[h, m] = (jnp.where(even, other, 1.0) * fresh + mine * other * before).astype(BF16)
             e_copy(h, m).start()
 
-        @pl.when(even)
+        ubf[h, m] = jnp.where(even, mine * before + fresh, before).astype(BF16)
+        u_copy(h, m).start()
+        return carry
+
+    def relay_late(unit, carry):
+        h = lax.div(unit, mems)
+        m = lax.rem(unit, mems)
+        mine, other = atot[pl.ds(unit, 1), :], apart[pl.ds(unit, 1), :]
+        u_copy(h, m).wait_recv()
+
+        @pl.when(m < direct)
         def _():
-            sgrp[h, m] = erecv[h, m]
-
-        @pl.when(jnp.logical_not(even))
+            receive(h, m)
+
+            @pl.when(jnp.logical_not(last))
+            def _():
+                both = jnp.where(even, other, 1.0) * u32[h, m]
+                both = both + jnp.where(even, 1.0, mine) * upart[h, m].astype(F32)
+                esend[h, m] = (both + mine * other * erecv[h, m].astype(F32)).astype(BF16)
+                e_copy(h, m).start()
+
+            @pl.when(even)
+            def _():
+                sgrp[h, m] = erecv[h, m]
+
+            @pl.when(jnp.logical_not(even))
+            def _():
+                sgrp[h, m] = (other * erecv[h, m].astype(F32) + upart[h, m].astype(F32)).astype(BF16)
+
+        @pl.when(m >= direct)
         def _():
-            sgrp[h, m] = (other * erecv[h, m].astype(F32) + upart[h, m].astype(F32)).astype(BF16)
+            sgrp[h, m] = (jnp.where(even, 1.0, other) * erecv[h, m].astype(F32)
+                          + upart[h, m].astype(F32)).astype(BF16)
 
         return carry
 
@@ -287,18 +314,24 @@
             mixed = mixed + wide[j, 2 + r] * (part * scale).astype(BF16).astype(F32)
         outb[h, j] = (mixed * gain).astype(BF16)
 
-    done = [0]
+    done = [0, 0]
 
     def catch_up(now, low, high):
-        upto = jnp.clip(lax.div(now - RELAY_AT - rank * HOP + 100 * RELAY_STEP, RELAY_STEP) - 99,
-                        low * mems, high * mems)
-        lax.fori_loop(done[0], upto, relay, 0)
-        done[0] = upto
+        for stage, per, start in ((0, turned_later, EARLY_AT), (1, mems, LATE_AT)):
+            since = now - start - rank * HOP + (64 + seqs) * HEAD_STEP
+            whole = lax.div(since, HEAD_STEP)
+            some = jnp.minimum(lax.div(since - whole * HEAD_STEP, PIECE_STEP) + 1, per)
+            upto = jnp.clip((whole - 64 - seqs) * per + some, low * per, high * per)
+            upto = jnp.maximum(upto, done[stage])
+            lax.fori_loop(done[stage], upto, (relay_early, relay_late)[stage], 0)
+            done[stage] = upto
 
     for h in range(hl):
         update(h)
+        if h == 0:
+            a_copy().wait_recv()
         now = KEYS_AT + h * HEAD_STEP + UPDATE_NS
-        catch_up(now, 0, h)
+        catch_up(now, 0, h + 1)
         own_token(2, h).wait()
         token_copy(2, h, near[0], near[0]).wait_recv()
         for j in [me] + near:
@@ -360,7 +393,7 @@
     vm = pltpu.VMEM
     dma = pltpu.SemaphoreType.DMA
     rows = hl * mems
-    scratch = [
+    buffers = [
         vm((n, hl, tok, hd), BF16), vm((n, hl, tok, hd), BF16), vm((n, hl, tok, hd), BF16),
         vm((n, heads, tok), BF16), vm((n, 2, tok), jnp.int32), vm((n, 2, tok), F32),
         vm(rate.shape, BF16), vm((1, feats), F32),
@@ -372,9 +405,13 @@
         vm((hl, mems, hd, hd), BF16), vm((hl, mems, hd, hd), BF16), vm((hl, mems, hd, hd), BF16),
         vm((hl, n, 2 * tok, hd), F32),
         vm((hl, n, tok, hd), BF16),
+    ]
+    scratch = buffers + [
         dma((3, n)), dma((3, n)), dma((3, hl, n)), dma((3, hl, n)), dma((2,)), dma, dma,
         dma((hl, mems)), dma((hl, mems)), dma((hl, mems)), dma((hl, mems)), dma((hl, n)), dma((hl, n)), dma((hl,)),
     ]
+    held = sum(math.prod(x.shape) * jnp.dtype(x.dtype).itemsize for x in buffers)
+    grant = min(held + held // 8 + (12 << 20), 60 << 20)
     spec = pl.BlockSpec(memory_space=pl.ANY)
     return pl.pallas_call(
         functools.partial(kernel, n, seqs, hl, mems, pair),
@@ -383,8 +420,8 @@
         out_specs=spec,
         scratch_shapes=scratch,
         compiler_params=pltpu.CompilerParams(
-            collective_id=0, has_side_effects=True, vmem_limit_bytes=60 * 1024 * 1024),
-    )(queries, keys, values, gamma.T, rate, route_ids.T, route_weights.T, norm_gain.reshape(1, feats))
+            collective_id=0, has_side_effects=True, vmem_limit_bytes=grant),
+    )(*[pltpu.with_memory_space_constraint(x, pltpu.HBM) for x in (queries, keys, values, gamma.T, rate, route_ids.T, route_weights.T, norm_gain.reshape(1, feats))])
 
 
 def solution(mesh):

time: 39.6 us -> 35.9 us (0.907)
  Pallas kernels: 37.5 us -> 34.9 us
  local copies, waits for them, and re-layouts: 1.88 us -> 0.8 us
    pallas_call x1, Pallas kernels: 37.5 us -> 34.9 us  [body(): pl.pallas_call(functools.partial(kernel, n, seqs, hl, mems, pair), out_sh...]
    unnamed x1, local copies, waits for them, and re-layouts: 1.88 us -> 0.8 us
where the time goes in v2:
time: 35.9 us; the launch traced here: 35.8 us
  Pallas kernels  34.9 us (97%)
  local copies, waits for them, and re-layouts  0.8 us (2%)
    pallas_call x1, Pallas kernels, body(): pl.pallas_call(functools.partial(kernel, n, seqs, hl, mems, pair), out_sh...  34.9 us
    unnamed x1, local copies, waits for them, and re-layouts  0.8 us

profile of v2, /device:TPU:29, one launch (start us, length us, event | category | flops | bytes accessed | tf_op | source)
XLA Modules:
  0.0 35.8 jit_solution(13095532545840760093)
XLA Ops:
  0.0 34.9 %shard_map.82 = bf16[128,2048]{1,0:T(8,128)(2,1)S(1)} custom-call(bf16[128,2048]{1,0:T(8,128)(2,1)} %q_ref.1, bf16[128,2048]{1,0:T(8,128)(2,1)} %k_ref.1, bf16[128,2048]{1,0:T(8,128)(2,1)} %v_ref.1, bf16[16,128]{1,0:T(8,128)(2,1)} %bitcast.5, bf16[4,16]{1,0:T(4,128)(2,1)} %rate_ref.1, s32[2,128]{1,0:T(2,128)} %bitcast.6, f32[2,128]{1,0:T(2,128)} %bitcast.7, ...), custom_call_target="tpu_custom_call" | custom-call | tf_op jit(solution)/shard_map/pallas_call | solution.py:416
  35.0 0.8 %copy.10 = bf16[128,2048]{1,0:T(8,128)(2,1)} copy(bf16[128,2048]{1,0:T(8,128)(2,1)S(1)} %shard_map.82) | data formatting | bytes 1048576

commit v3 on v2

--- a/solution.py
+++ b/solution.py
@@ -18,7 +18,7 @@
 HEAD_STEP = 2860
 QUERY_STEP = 1430
 EARLY_AT = 8850
-LATE_AT = 12000
+LATE_AT = 11700
 PIECE_STEP = 700
 HOP = 1900
 UPDATE_NS = 450
@@ -219,8 +219,10 @@
         for m in range(mems):
             u32[h, m] = state[m * hd:(m + 1) * hd]
             if m < direct:
-                ubf[h, m] = state[m * hd:(m + 1) * hd].astype(BF16)
-                u_copy(h, m).start()
+                @pl.when(jnp.logical_or(even, jnp.logical_not(last)))
+                def _():
+                    ubf[h, m] = state[m * hd:(m + 1) * hd].astype(BF16)
+                    u_copy(h, m).start()
 
     causal = row_at >= col_at
 
@@ -267,15 +269,22 @@
             esend[h, m] = (jnp.where(even, other, 1.0) * fresh + mine * other * before).astype(BF16)
             e_copy(h, m).start()
 
-        ubf[h, m] = jnp.where(even, mine * before + fresh, before).astype(BF16)
-        u_copy(h, m).start()
+        @pl.when(jnp.logical_or(even, jnp.logical_not(first)))
+        def _():
+            ubf[h, m] = jnp.where(even, mine * before + fresh, before).astype(BF16)
+            u_copy(h, m).start()
+
         return carry
 
     def relay_late(unit, carry):
         h = lax.div(unit, mems)
         m = lax.rem(unit, mems)
         mine, other = atot[pl.ds(unit, 1), :], apart[pl.ds(unit, 1), :]
-        u_copy(h, m).wait_recv()
+        unsent = jnp.logical_and(even, jnp.where(m < direct, last, first))
+
+        @pl.when(jnp.logical_not(unsent))
+        def _():
+            u_copy(h, m).wait_recv()
 
         @pl.when(m < direct)
         def _():
@@ -296,7 +305,11 @@
             def _():
                 sgrp[h, m] = (other * erecv[h, m].astype(F32) + upart[h, m].astype(F32)).astype(BF16)
 
-        @pl.when(m >= direct)
+        @pl.when(jnp.logical_and(m >= direct, unsent))
+        def _():
+            sgrp[h, m] = jnp.zeros((hd, hd), BF16)
+
+        @pl.when(jnp.logical_and(m >= direct, jnp.logical_not(unsent)))
         def _():
             sgrp[h, m] = (jnp.where(even, 1.0, other) * erecv[h, m].astype(F32)
                           + upart[h, m].astype(F32)).astype(BF16)
@@ -376,7 +389,9 @@
     a_copy().wait_send()
     for h in range(hl):
         for m in range(mems):
-            u_copy(h, m).wait_send()
+            @pl.when(jnp.logical_or(even, jnp.logical_not(last if m < direct else first)))
+            def _():
+                u_copy(h, m).wait_send()
 
             @pl.when(jnp.logical_not(last))
             def _():

time: 35.9 us -> 36.2 us (level)
  no operation moved by 1% of the time
where the time goes in v3:
time: 36.2 us; the launch traced here: 36 us
  Pallas kernels  35.2 us (97%)
  local copies, waits for them, and re-layouts  0.8 us (2%)
    pallas_call x1, Pallas kernels, body(): pl.pallas_call(functools.partial(kernel, n, seqs, hl, mems, pair), out_sh...  35.2 us
    unnamed x1, local copies, waits for them, and re-layouts  0.8 us

profile of v3, /device:TPU:29, one launch (start us, length us, event | category | flops | bytes accessed | tf_op | source)
XLA Modules:
  0.0 36.0 jit_solution(16929533724682482151)
XLA Ops:
  0.0 35.2 %shard_map.82 = bf16[128,2048]{1,0:T(8,128)(2,1)S(1)} custom-call(bf16[128,2048]{1,0:T(8,128)(2,1)} %q_ref.1, bf16[128,2048]{1,0:T(8,128)(2,1)} %k_ref.1, bf16[128,2048]{1,0:T(8,128)(2,1)} %v_ref.1, bf16[16,128]{1,0:T(8,128)(2,1)} %bitcast.5, bf16[4,16]{1,0:T(4,128)(2,1)} %rate_ref.1, s32[2,128]{1,0:T(2,128)} %bitcast.6, f32[2,128]{1,0:T(2,128)} %bitcast.7, ...), custom_call_target="tpu_custom_call" | custom-call | tf_op jit(solution)/shard_map/pallas_call | solution.py:431
  35.2 0.8 %copy.10 = bf16[128,2048]{1,0:T(8,128)(2,1)} copy(bf16[128,2048]{1,0:T(8,128)(2,1)S(1)} %shard_map.82) | data formatting | bytes 1048576
